TPU v7x, 32 devices: a whole 2x2x4 slice. The times are simulated.
32 devices in a mesh: band: 4 (over y, x), chan: 8 (over z, core).
Axes of the slice: x: 2, y: 2, z: 4, core: 2. Of those that a mesh axis runs over, the one named last changes fastest.
Arguments:
- coeffs: bfloat16 [2, 8, 1024, 4096], P(None, None, 'chan', 'band'), may hold values from -1100 to 1100, as said below
Outputs:
- coherence: float32 [1024, 1024], P('chan', 'band')
Inputs may be any that keep to these rules, and one draw needn't show every extreme that they name: `coeffs`: finite real and imaginary parts.
All inputs are finite; a program needn't handle non-finite values.
Results may differ from a plain program's by a relative error of at most 0.0003.
Values may be sent and summed in bfloat16 or wider, within the bound.
A program may use at most 192 MiB of HBM per device.

v0:
```python
import jax
import jax.numpy as jnp
from jax import lax
from jax.sharding import PartitionSpec as P

K = 8
W = 16


epsilon = 1e-06


def from_behind(block, axis, distance):
    devices = range(lax.axis_size(axis))
    route = [((i - distance) % len(devices), i) for i in devices]
    return lax.ppermute(block, axis, route)


def body(coeffs):
    num_bands = coeffs.shape[3] // W
    own_width = coeffs.shape[2]
    cycle_size = lax.axis_size("chan")
    own_index = lax.axis_index("chan")
    full_width = own_width * cycle_size
    group_count = lax.axis_size("band")
    share_width = full_width // group_count
    scale = jnp.float32(W * K / (num_bands * group_count))
    local_rows = coeffs.reshape(2, K, own_width, num_bands, W)
    paired = jnp.stack((local_rows[1], -local_rows[0]), axis=0)
    left_side = jnp.concatenate((local_rows, paired), axis=2)
    wide_rows = local_rows.astype(jnp.float32)
    own_power = jnp.sum(wide_rows * wide_rows, axis=(0, 1, 4)).T + epsilon

    def block_coherence(piece):
        count = piece.shape[2]
        right_side = piece.reshape(2, K, count, num_bands, W)
        product = jnp.einsum(
            "pkinw,pkjnw->nij", left_side, right_side, preferred_element_type=jnp.float32
        )
        real_part = product[:, :own_width, :]
        imag_part = product[:, own_width:, :]
        wide_piece = right_side.astype(jnp.float32)
        piece_power = jnp.sum(wide_piece * wide_piece, axis=(0, 1, 4)).T + epsilon
        coh_band = (real_part * real_part + imag_part * imag_part) / (
            own_power[:, :, None] * piece_power[:, None, :]
        )
        return jnp.sum(coh_band, axis=0)

    empty = jnp.zeros((own_width, full_width), jnp.float32)
    first = lax.dynamic_update_slice(
        empty, block_coherence(coeffs), (jnp.int32(0), own_index * own_width)
    )

    def step_once(offset, carry):
        moving, partial_sum = carry
        moving = from_behind(moving, "chan", 1)
        column = (own_index - offset) % cycle_size * own_width
        partial_sum = lax.dynamic_update_slice(
            partial_sum, block_coherence(moving), (jnp.int32(0), column)
        )
        return (moving, partial_sum)

    unused_block, partial_value = lax.fori_loop(1, cycle_size // 2 + 1, step_once, (coeffs, first))
    outgoing = partial_value.reshape(own_width, cycle_size, own_width).transpose(1, 2, 0)
    incoming = lax.all_to_all(outgoing, "chan", split_axis=0, concat_axis=0, tiled=True)
    mirrored = incoming.transpose(1, 0, 2).reshape(own_width, full_width)
    col_block = lax.broadcasted_iota(jnp.int32, (own_width, full_width), 1) // own_width
    computed = (own_index - col_block) % cycle_size <= cycle_size // 2
    partial_value = jnp.where(computed, partial_value, mirrored)
    row_global = lax.broadcasted_iota(jnp.int32, (own_width, full_width), 0) + own_index * own_width
    col_global = lax.broadcasted_iota(jnp.int32, (own_width, full_width), 1)
    partial_value = jnp.where(row_global == col_global, jnp.float32(0.0), partial_value)
    summed = lax.psum(partial_value, "band")
    result = lax.dynamic_slice_in_dim(summed, lax.axis_index("band") * share_width, share_width, 1)
    return result * scale


def solution(mesh):
    return jax.shard_map(
        body,
        mesh=mesh,
        in_specs=(P(None, None, "chan", "band"),),
        out_specs=P("chan", "band"),
        check_vma=False,
    )
```

profile of v0, /device:TPU:0, one launch (start us, length us, event | category | flops | bytes accessed | tf_op | source)
XLA Modules:
  0.0 404.4 jit_solution(6095935541192641976)
XLA Ops:
  6.5 6.2 %copy.49 = bf16[2,8,128,1024]{2,3,1,0:T(8,128)(2,1)} copy(bf16[2,8,128,1024]{3,2,1,0:T(8,128)(2,1)} %param.3) | data formatting | bytes 8388608 | tf_op jit(solution)/shard_map/while | solution.py:63
  12.7 0.0 copy-start
  12.7 4.2 %multiply_reduce_fusion.1 = f32[128,1024]{1,0:T(8,128)} fusion(bf16[2,8,128,1024]{3,2,1,0:T(8,128)(2,1)} %param.3), kind=kLoop, calls=%fused_computation.13 | loop fusion | flops 6160384 | bytes 4718592 | tf_op jit(solution)/shard_map/reduce_sum | solution.py:32
  16.9 0.0 copy-done
  16.9 1.7 fusion.18
  18.7 5.8 %convolution_bitcast_fusion = f32[64,256,128]{2,1,0:T(8,128)} fusion(bf16[2,8,128,64,16]{2,4,3,1,0:T(8,128)(2,1)S(1)} %bitcast.44, bf16[1,8,128,64,16]{2,4,0,3,1:T(8,128)(2,1)} %bitcast.48, bf16[1,8,128,64,16]{2,4,0,3,1:T(8,128)(2,1)S(1)} %bitcast.46), kind=kOutput, calls=%fused_computation.19 | convolution fusion | flops 1098907648 | bytes 16777216 | tf_op jit(solution)/shard_map/pkinw,pkjnw->nij/dot_general | solution.py:37
  24.5 5.8 %maximum_maximum_fusion = bf16[2,8,256,64,16]{2,4,0,3,1:T(8,128)(2,1)} fusion(bf16[1,8,128,64,16]{2,4,0,3,1:T(8,128)(2,1)} %bitcast.49, bf16[1,8,128,64,16]{2,4,0,3,1:T(8,128)(2,1)S(1)} %bitcast.47, bf16[2,8,128,64,16]{2,4,3,1,0:T(8,128)(2,1)S(1)} %bitcast.45), kind=kLoop, calls=%fused_computation.12 | loop fusion | flops 25165824 | bytes 16777216 | tf_op jit(solution)/shard_map/concatenate | solution.py:30
  30.2 1.2 copy.47
  31.5 0.1 bitcast_reduce_fusion.1
  31.6 4.1 %fusion.10 = f32[128,128]{1,0:T(8,128)S(1)} fusion(f32[64,256,128]{2,1,0:T(8,128)} %convolution_bitcast_fusion, f32[64,128]{1,0:T(8,128)S(1)} %add_bitcast_fusion.1), kind=kLoop, calls=%fused_computation.18 | loop fusion | flops 6275072 | bytes 8519680 | tf_op jit(solution)/shard_map/reduce_sum | solution.py:47
  35.7 0.1 copy.48
  35.8 0.9 broadcast_in_dim.13
  36.7 0.6 constant_dynamic-update-slice_fusion.1
  37.3 292.1 %while.17 = (s32[]{:T(128)}, bf16[2,8,128,1024]{2,3,1,0:T(8,128)(2,1)}, f32[128,1024]{0,1:T(8,128)}, bf16[2,8,256,64,16]{2,4,0,3,1:T(8,128)(2,1)}, f32[64,128]{1...) while((s32[]{:T(128)}, ...), condition=%wide.region_7.8_spmd, body=%wide.region_3.7_spmd.sunk | while | flops 1086308352 | bytes 60260672 | solution.py:63
  37.4 0.5 collective-permute-start
  37.8 50.5 %collective-permute-done = bf16[2,8,128,1024]{2,3,1,0:T(8,128)(2,1)} collective-permute-done((bf16[2,8,128,1024]{2,3,1,0:T(8,128)(2,1)}, bf16[2,8,128,1024]{2,3,1,0:T(8,128)(2,1)}, u32[]{:S(2)}, u32[]{:S(2)}) %collective-permute-start) | collective-permute-done | bytes 4194336 | tf_op jit(solution)/shard_map/while/body/eval_jaxpr/ppermute | solution.py:16
  88.4 3.1 multiply_reduce_fusion.3
  91.4 0.1 bitcast_reduce_fusion.3
  91.5 10.2 %fusion.28 = f32[64,256,128]{2,1,0:T(8,128)} fusion(bf16[2,8,256,64,16]{2,4,0,3,1:T(8,128)(2,1)} %get-tuple-element.265, bf16[2,8,128,64,16]{2,4,3,1,0:T(8,128)(2,1)} %bitcast.43), kind=kOutput, calls=%fused_computation.8.clone.1 | convolution fusion | flops 1073741824 | bytes 20971520 | tf_op jit(solution)/shard_map/while/body/eval_jaxpr/pkinw,pkjnw->nij/dot_general | solution.py:37
  101.7 4.1 %fusion.29 = f32[128,128]{1,0:T(8,128)S(1)} fusion(f32[64,256,128]{2,1,0:T(8,128)} %fusion.28, f32[64,128]{1,0:T(8,128)S(1)} %add_bitcast_fusion.3, f32[64,128]{1,0:T(8,128)S(1)} %get-tuple-element.266), kind=kLoop, calls=%fused_computation.7.clone.1 | loop fusion | flops 6275072 | bytes 8519680 | tf_op jit(solution)/shard_map/while/body/eval_jaxpr/reduce_sum | solution.py:47
  105.9 0.1 copy.73
  105.9 0.6 constant_dynamic-update-slice_fusion.3
  106.6 4.5 %copy.83 = bf16[2,8,128,1024]{2,3,1,0:T(8,128)(2,1)} copy(bf16[2,8,128,1024]{2,3,1,0:T(8,128)(2,1)} %collective-permute-done) | data formatting | bytes 8388608 | tf_op jit(solution)/shard_map/while
  111.1 0.0 collective-permute-start
  111.1 50.0 %collective-permute-done = bf16[2,8,128,1024]{2,3,1,0:T(8,128)(2,1)} collective-permute-done((bf16[2,8,128,1024]{2,3,1,0:T(8,128)(2,1)}, bf16[2,8,128,1024]{2,3,1,0:T(8,128)(2,1)}, u32[]{:S(2)}, u32[]{:S(2)}) %collective-permute-start) | collective-permute-done | bytes 4194336 | tf_op jit(solution)/shard_map/while/body/eval_jaxpr/ppermute | solution.py:16
  161.1 3.1 multiply_reduce_fusion.3
  164.2 0.1 bitcast_reduce_fusion.3
  164.3 10.2 %fusion.28 = f32[64,256,128]{2,1,0:T(8,128)} fusion(bf16[2,8,256,64,16]{2,4,0,3,1:T(8,128)(2,1)} %get-tuple-element.265, bf16[2,8,128,64,16]{2,4,3,1,0:T(8,128)(2,1)} %bitcast.43), kind=kOutput, calls=%fused_computation.8.clone.1 | convolution fusion | flops 1073741824 | bytes 20971520 | tf_op jit(solution)/shard_map/while/body/eval_jaxpr/pkinw,pkjnw->nij/dot_general | solution.py:37
  174.5 4.1 %fusion.29 = f32[128,128]{1,0:T(8,128)S(1)} fusion(f32[64,256,128]{2,1,0:T(8,128)} %fusion.28, f32[64,128]{1,0:T(8,128)S(1)} %add_bitcast_fusion.3, f32[64,128]{1,0:T(8,128)S(1)} %get-tuple-element.266), kind=kLoop, calls=%fused_computation.7.clone.1 | loop fusion | flops 6275072 | bytes 8519680 | tf_op jit(solution)/shard_map/while/body/eval_jaxpr/reduce_sum | solution.py:47
  178.6 0.1 copy.73
  178.7 0.6 constant_dynamic-update-slice_fusion.3
  179.4 4.5 %copy.83 = bf16[2,8,128,1024]{2,3,1,0:T(8,128)(2,1)} copy(bf16[2,8,128,1024]{2,3,1,0:T(8,128)(2,1)} %collective-permute-done) | data formatting | bytes 8388608 | tf_op jit(solution)/shard_map/while
  183.9 0.0 collective-permute-start
  183.9 50.0 %collective-permute-done = bf16[2,8,128,1024]{2,3,1,0:T(8,128)(2,1)} collective-permute-done((bf16[2,8,128,1024]{2,3,1,0:T(8,128)(2,1)}, bf16[2,8,128,1024]{2,3,1,0:T(8,128)(2,1)}, u32[]{:S(2)}, u32[]{:S(2)}) %collective-permute-start) | collective-permute-done | bytes 4194336 | tf_op jit(solution)/shard_map/while/body/eval_jaxpr/ppermute | solution.py:16
  233.9 3.1 multiply_reduce_fusion.3
  237.0 0.1 bitcast_reduce_fusion.3
  237.1 10.2 %fusion.28 = f32[64,256,128]{2,1,0:T(8,128)} fusion(bf16[2,8,256,64,16]{2,4,0,3,1:T(8,128)(2,1)} %get-tuple-element.265, bf16[2,8,128,64,16]{2,4,3,1,0:T(8,128)(2,1)} %bitcast.43), kind=kOutput, calls=%fused_computation.8.clone.1 | convolution fusion | flops 1073741824 | bytes 20971520 | tf_op jit(solution)/shard_map/while/body/eval_jaxpr/pkinw,pkjnw->nij/dot_general | solution.py:37
  247.3 4.1 %fusion.29 = f32[128,128]{1,0:T(8,128)S(1)} fusion(f32[64,256,128]{2,1,0:T(8,128)} %fusion.28, f32[64,128]{1,0:T(8,128)S(1)} %add_bitcast_fusion.3, f32[64,128]{1,0:T(8,128)S(1)} %get-tuple-element.266), kind=kLoop, calls=%fused_computation.7.clone.1 | loop fusion | flops 6275072 | bytes 8519680 | tf_op jit(solution)/shard_map/while/body/eval_jaxpr/reduce_sum | solution.py:47
  251.4 0.1 copy.73
  251.5 0.6 constant_dynamic-update-slice_fusion.3
  252.1 4.5 %copy.83 = bf16[2,8,128,1024]{2,3,1,0:T(8,128)(2,1)} copy(bf16[2,8,128,1024]{2,3,1,0:T(8,128)(2,1)} %collective-permute-done) | data formatting | bytes 8388608 | tf_op jit(solution)/shard_map/while
  256.6 0.0 collective-permute-start
  256.7 50.0 %collective-permute-done = bf16[2,8,128,1024]{2,3,1,0:T(8,128)(2,1)} collective-permute-done((bf16[2,8,128,1024]{2,3,1,0:T(8,128)(2,1)}, bf16[2,8,128,1024]{2,3,1,0:T(8,128)(2,1)}, u32[]{:S(2)}, u32[]{:S(2)}) %collective-permute-start) | collective-permute-done | bytes 4194336 | tf_op jit(solution)/shard_map/while/body/eval_jaxpr/ppermute | solution.py:16
  306.7 3.1 multiply_reduce_fusion.3
  309.8 0.1 bitcast_reduce_fusion.3
  309.9 10.2 %fusion.28 = f32[64,256,128]{2,1,0:T(8,128)} fusion(bf16[2,8,256,64,16]{2,4,0,3,1:T(8,128)(2,1)} %get-tuple-element.265, bf16[2,8,128,64,16]{2,4,3,1,0:T(8,128)(2,1)} %bitcast.43), kind=kOutput, calls=%fused_computation.8.clone.1 | convolution fusion | flops 1073741824 | bytes 20971520 | tf_op jit(solution)/shard_map/while/body/eval_jaxpr/pkinw,pkjnw->nij/dot_general | solution.py:37
  320.0 4.1 %fusion.29 = f32[128,128]{1,0:T(8,128)S(1)} fusion(f32[64,256,128]{2,1,0:T(8,128)} %fusion.28, f32[64,128]{1,0:T(8,128)S(1)} %add_bitcast_fusion.3, f32[64,128]{1,0:T(8,128)S(1)} %get-tuple-element.266), kind=kLoop, calls=%fused_computation.7.clone.1 | loop fusion | flops 6275072 | bytes 8519680 | tf_op jit(solution)/shard_map/while/body/eval_jaxpr/reduce_sum | solution.py:47
  324.2 0.1 copy.73
  324.3 0.6 constant_dynamic-update-slice_fusion.3
  324.9 4.5 %copy.83 = bf16[2,8,128,1024]{2,3,1,0:T(8,128)(2,1)} copy(bf16[2,8,128,1024]{2,3,1,0:T(8,128)(2,1)} %collective-permute-done) | data formatting | bytes 8388608 | tf_op jit(solution)/shard_map/while
  329.4 3.5 all-to-all-start
  332.9 0.0 all-reduce.2.cloned.1.call-start
  333.0 15.2 %all-to-all-done = f32[8,128,128]{2,1,0:T(8,128)S(1)} async-done(((f32[8,128,128]{2,1,0:T(8,128)}), f32[8,128,128]{2,1,0:T(8,128)S(1)}, u32[]{:S(2)}, u32[]{:S(2)}) %all-to-all-start) | async-done | bytes 524320 | tf_op jit(solution)/shard_map/all_to_all | solution.py:65
  348.2 0.2 copy.52
  348.4 2.5 fusion.13
  350.9 0.0 all-reduce.2.cloned.1.call-update
  350.9 44.9 %all-reduce.2.cloned.1.call-done = f32[128,1024]{0,1:T(8,128)} async-done(((f32[128,1024]{0,1:T(8,128)}), f32[128,1024]{0,1:T(8,128)}) %all-reduce.2.cloned.1.call-update) | async-done | bytes 524304 | tf_op jit(solution)/shard_map/psum | solution.py:73
  395.9 0.9 dynamic-slice_multiply_fusion
  396.8 0.8 copy.54
  (8 shorter events, 0.0 us)
Async XLA Ops:
  12.7 4.2 %copy-start = (bf16[2,8,128,1024]{2,3,1,0:T(8,128)(2,1)S(1)}, bf16[2,8,128,1024]{2,3,1,0:T(8,128)(2,1)}, u32[]{:S(2)}) copy-start(bf16[2,8,128,1024]{2,3,1,0:T(8,128)(2,1)} %copy.49) | copy-start | bytes 12582916
  37.4 51.0 %collective-permute-start = (bf16[2,8,128,1024]{2,3,1,0:T(8,128)(2,1)}, bf16[2,8,128,1024]{2,3,1,0:T(8,128)(2,1)}, u32[]{:S(2)}, u32[]{:S(2)}) collective-permute-start(bf16[2,8,128,1024]{2,3,1,0:T(8,128)(2,1)} %get-tuple-element.251), channel_id=1, source_target_pairs={{7,0},{0,1},{1,2},{2,3},{3,4},{4,5},{5,6},{6,7},{15,8},{8,9},{9,10... | collective-permute-start | bytes 12582920 | tf_op jit(solution)/shard_map/while/body/eval_jaxpr/ppermute | solution.py:16
  111.1 50.0 %collective-permute-start = (bf16[2,8,128,1024]{2,3,1,0:T(8,128)(2,1)}, bf16[2,8,128,1024]{2,3,1,0:T(8,128)(2,1)}, u32[]{:S(2)}, u32[]{:S(2)}) collective-permute-start(bf16[2,8,128,1024]{2,3,1,0:T(8,128)(2,1)} %get-tuple-element.251), channel_id=1, source_target_pairs={{7,0},{0,1},{1,2},{2,3},{3,4},{4,5},{5,6},{6,7},{15,8},{8,9},{9,10... | collective-permute-start | bytes 12582920 | tf_op jit(solution)/shard_map/while/body/eval_jaxpr/ppermute | solution.py:16
  183.9 50.0 %collective-permute-start = (bf16[2,8,128,1024]{2,3,1,0:T(8,128)(2,1)}, bf16[2,8,128,1024]{2,3,1,0:T(8,128)(2,1)}, u32[]{:S(2)}, u32[]{:S(2)}) collective-permute-start(bf16[2,8,128,1024]{2,3,1,0:T(8,128)(2,1)} %get-tuple-element.251), channel_id=1, source_target_pairs={{7,0},{0,1},{1,2},{2,3},{3,4},{4,5},{5,6},{6,7},{15,8},{8,9},{9,10... | collective-permute-start | bytes 12582920 | tf_op jit(solution)/shard_map/while/body/eval_jaxpr/ppermute | solution.py:16
  256.6 50.0 %collective-permute-start = (bf16[2,8,128,1024]{2,3,1,0:T(8,128)(2,1)}, bf16[2,8,128,1024]{2,3,1,0:T(8,128)(2,1)}, u32[]{:S(2)}, u32[]{:S(2)}) collective-permute-start(bf16[2,8,128,1024]{2,3,1,0:T(8,128)(2,1)} %get-tuple-element.251), channel_id=1, source_target_pairs={{7,0},{0,1},{1,2},{2,3},{3,4},{4,5},{5,6},{6,7},{15,8},{8,9},{9,10... | collective-permute-start | bytes 12582920 | tf_op jit(solution)/shard_map/while/body/eval_jaxpr/ppermute | solution.py:16
  329.4 18.8 %all-to-all-start = ((f32[8,128,128]{2,1,0:T(8,128)}), f32[8,128,128]{2,1,0:T(8,128)S(1)}, u32[]{:S(2)}, u32[]{:S(2)}) async-start(f32[8,128,128]{2,1,0:T(8,128)} %bitcast.17), calls=%async_computation | async-start | bytes 1048576 | tf_op jit(solution)/shard_map/all_to_all | solution.py:65
  332.9 63.0 %all-reduce.2.cloned.1.call-start = ((), (), s32[]{:S(2)}) async-start(), calls=%async_computation.1 | async-start | bytes 1048576 | tf_op jit(solution)/shard_map/psum | solution.py:73
Sparse Core Ops, SparseCore 0:
  351.1 44.7 all-reduce.1
where the time goes:
time: 405 us; the launch traced here: 404 us
  waiting for transfers between devices  261 us (64%)
  other arithmetic  48.5 us (12%)
  matrix products  46.5 us (11%)
  local copies, waits for them, and re-layouts  30.9 us (8%)
  between operations  13.5 us (3%)
    ppermute x4, waiting for transfers between devices, from_behind(): return lax.ppermute(block, axis, route)  201 us
    dot_general x5, matrix products, block_coherence(): jnp.einsum('pkinw,pkjnw->nij', left_side, right_side, preferred_element_t...  46.5 us
    psum x1, waiting for transfers between devices, body(): summed = lax.psum(partial_value, 'band')  44.9 us
    reduce_sum x5, other arithmetic, block_coherence(): return jnp.sum(coh_band, axis=0)  20.7 us
    while x4, local copies, waits for them, and re-layouts  18.1 us
    all_to_all x1, waiting for transfers between devices, body(): lax.all_to_all(outgoing, 'chan', split_axis=0, concat_axis=0, tiled=True)  15.2 us
    reduce_sum x8, other arithmetic, block_coherence(): piece_power = jnp.sum(wide_piece * wide_piece, axis=(0, 1, 4)).T + epsilon  12.6 us
  transfers between devices with their start and end apart: 6, of which 6 were waited for; matrix products, arithmetic and copies ran while one was open for 0% of the time, Pallas kernels for 0%

commit v1 on v0

v1 whole, which is shorter than its diff:
```python
import functools

import jax
import jax.numpy as jnp
from jax import lax
from jax.experimental import pallas as pl
from jax.experimental.pallas import tpu as pltpu
from jax.sharding import PartitionSpec as P

W = 16

epsilon = 1e-06

MESH = pl.DeviceIdType.MESH


def partner(index, size, offset):
    other = index
    bit = 1
    while bit < size:
        if offset & bit:
            other = other + (1 - 2 * ((index // bit) % 2)) * bit
        bit *= 2
    return other


def kernel(x_ref, out_ref, buf, sel, xb, xq, inv_col, inv_row, own_sem, send_sem, recv_sem):
    n = lax.axis_size("chan")
    me = lax.axis_index("chan")
    parts, tapers, own, wide = buf.shape[1:]
    bands, full, depth = xb.shape
    lanes = bands * W
    half = depth // 2
    tile = min(256, full)

    def window(device):
        return pl.ds(pl.multiple_of(device * lanes // wide * wide, wide), wide)

    barrier = pltpu.get_barrier_semaphore()
    for offset in range(1, n):
        pl.semaphore_signal(
            barrier, inc=1, device_id={"chan": partner(me, n, offset)}, device_id_type=MESH
        )

    local = pltpu.make_async_copy(
        x_ref.at[:, :, :, window(me)], buf.at[me], own_sem
    )
    local.start()
    pl.semaphore_wait(barrier, n - 1)

    copies = {}
    for offset in reversed(range(1, n)):
        peer = partner(me, n, offset)
        copies[offset] = pltpu.make_async_remote_copy(
            src_ref=x_ref.at[:, :, :, window(peer)],
            dst_ref=buf.at[me],
            send_sem=send_sem.at[offset],
            recv_sem=recv_sem.at[offset],
            device_id={"chan": peer},
            device_id_type=MESH,
        )
        copies[offset].start()

    row = lax.broadcasted_iota(jnp.int32, (wide, bands * half), 0) - (me * lanes) % wide
    col = lax.broadcasted_iota(jnp.int32, (wide, bands * half), 1)
    band, within = col // half, col % half
    for k in range(tapers):
        hit = (row == band * W + within - k * W) & (within // W == k)
        sel[k * wide : (k + 1) * wide, :] = jnp.where(hit, 1.0, 0.0).astype(jnp.bfloat16)

    def relayout(src):
        rows = pl.ds(pl.multiple_of(src * own, own), own)
        re = jnp.concatenate([buf[src, 0, k] for k in range(tapers)], axis=1)
        im = jnp.concatenate([buf[src, 1, k] for k in range(tapers)], axis=1)
        lane = lax.broadcasted_iota(jnp.int32, (own, 128), 1)
        power = jnp.ones((own, 128), jnp.float32)
        for b in range(bands):
            chosen = sel[:, b * half : (b + 1) * half]
            re_b = jnp.dot(re, chosen, preferred_element_type=jnp.float32)
            im_b = jnp.dot(im, chosen, preferred_element_type=jnp.float32)
            total = jnp.sum(re_b * re_b + im_b * im_b, axis=1, keepdims=True) + epsilon
            power = jnp.where(lane == b, total, power)
            xb[b, rows, :half] = re_b.astype(jnp.bfloat16)
            xb[b, rows, half:] = im_b.astype(jnp.bfloat16)
            xq[b, rows, :half] = im_b.astype(jnp.bfloat16)
            xq[b, rows, half:] = (-re_b).astype(jnp.bfloat16)
        inv_col[rows, :] = 1.0 / power

    local.wait()
    relayout(me)
    for offset in range(1, n):
        copies[offset].wait_recv()
        relayout(partner(me, n, offset))

    count = full // tile
    for i in range(count):
        turned = inv_col[i * tile : (i + 1) * tile, :].T
        inv_row[:, i * tile : (i + 1) * tile] = turned[:bands, :]

    contract = (((1,), (1,)), ((), ()))
    for i in range(count):
        row0 = i * tile

        def column(j, carry):
            col0 = pl.multiple_of(j * tile, tile)
            acc = jnp.zeros((tile, tile), jnp.float32)
            for b in range(bands):
                right = xb[b, pl.ds(col0, tile), :]
                re = lax.dot_general(
                    xb[b, row0 : row0 + tile, :], right, contract, preferred_element_type=jnp.float32
                )
                im = lax.dot_general(
                    xq[b, row0 : row0 + tile, :], right, contract, preferred_element_type=jnp.float32
                )
                acc += ((re * re + im * im) * inv_col[row0 : row0 + tile, b : b + 1]) * inv_row[
                    b : b + 1, pl.ds(col0, tile)
                ]
            out_ref[row0 : row0 + tile, pl.ds(col0, tile)] = acc
            out_ref[pl.ds(col0, tile), row0 : row0 + tile] = acc.T
            return carry

        lax.fori_loop(i, count, column, 0)

    for offset in range(1, n):
        copies[offset].wait_send()


def body(coeffs):
    parts, tapers, own, bins = coeffs.shape
    n = lax.axis_size("chan")
    groups = lax.axis_size("band")
    full = own * n
    lanes = bins // n
    wide = max(lanes, 128)
    bands = lanes // W
    depth = parts * tapers * W
    scale = jnp.float32(W * tapers / (bins // W * groups))
    partial_sum = pl.pallas_call(
        kernel,
        out_shape=jax.ShapeDtypeStruct((full, full), jnp.float32),
        in_specs=[pl.BlockSpec(memory_space=pl.ANY)],
        out_specs=pl.BlockSpec(memory_space=pltpu.VMEM),
        scratch_shapes=[
            pltpu.VMEM((n, parts, tapers, own, wide), jnp.bfloat16),
            pltpu.VMEM((tapers * wide, bands * tapers * W), jnp.bfloat16),
            pltpu.VMEM((bands, full, depth), jnp.bfloat16),
            pltpu.VMEM((bands, full, depth), jnp.bfloat16),
            pltpu.VMEM((full, 128), jnp.float32),
            pltpu.VMEM((bands, full), jnp.float32),
            pltpu.SemaphoreType.DMA,
            pltpu.SemaphoreType.DMA((n,)),
            pltpu.SemaphoreType.DMA((n,)),
        ],
        compiler_params=pltpu.CompilerParams(
            collective_id=0, has_side_effects=True, vmem_limit_bytes=48 * 1024 * 1024
        ),
    )(coeffs)
    summed = lax.psum_scatter(partial_sum, "band", scatter_dimension=1, tiled=True)
    summed = lax.psum_scatter(summed, "chan", scatter_dimension=0, tiled=True)
    share = full // groups
    row_global = lax.broadcasted_iota(jnp.int32, (own, share), 0) + lax.axis_index("chan") * own
    col_global = lax.broadcasted_iota(jnp.int32, (own, share), 1) + lax.axis_index("band") * share
    return jnp.where(row_global == col_global, jnp.float32(0.0), summed) * scale


def solution(mesh):
    return jax.shard_map(
        body,
        mesh=mesh,
        in_specs=(P(None, None, "chan", "band"),),
        out_specs=P("chan", "band"),
        check_vma=False,
    )
```

time: 405 us -> 216 us (0.53)
  waiting for transfers between devices: 261 us -> 87.6 us
  Pallas kernels: 0 us -> 111 us
  other arithmetic: 48.5 us -> 1.65 us
  matrix products: 46.5 us -> 0 us
  local copies, waits for them, and re-layouts: 30.9 us -> 1.93 us
    ppermute x4 -> x0, waiting for transfers between devices: 201 us -> none  [from_behind(): return lax.ppermute(block, axis, route)]
    pallas_call x0 -> x1, Pallas kernels: none -> 111 us  [body(): pl.pallas_call(kernel, out_shape=jax.ShapeDtypeStruct((full, full), jnp.f...]
    reduce_scatter x0 -> x2, waiting for transfers between devices: none -> 87.6 us  [the longest x1 52.8 us: body(): lax.psum_scatter(partial_sum, 'band', scatter_dimension=1, tiled=True)]
    dot_general x5 -> x0, matrix products: 46.5 us -> none  [block_coherence(): jnp.einsum('pkinw,pkjnw->nij', left_side, right_side, preferred_element_t...]
    psum x1 -> x0, waiting for transfers between devices: 44.9 us -> none  [body(): summed = lax.psum(partial_value, 'band')]
    reduce_sum x15 -> x0, other arithmetic: 37.6 us -> none  [the longest x5 20.7 us: block_coherence(): return jnp.sum(coh_band, axis=0)]
    while x5 -> x0, local copies, waits for them, and re-layouts: 24.3 us -> none
    all_to_all x1 -> x0, waiting for transfers between devices: 15.2 us -> none  [body(): lax.all_to_all(outgoing, 'chan', split_axis=0, concat_axis=0, tiled=True)]
  transfers between devices with their start and end apart: 6 -> 2, of which waited for: 6 -> 2; matrix products, arithmetic and copies ran while one was open for 0% -> 0% of each run, Pallas kernels for 0% -> 0%
where the time goes in v1:
time: 216 us
  Pallas kernels  111 us (51%)
  waiting for transfers between devices  87.6 us (41%)
  between operations  13.4 us (6%)
    pallas_call x1, Pallas kernels, body(): pl.pallas_call(kernel, out_shape=jax.ShapeDtypeStruct((full, full), jnp.f...  111 us
    reduce_scatter x1, waiting for transfers between devices, body(): lax.psum_scatter(partial_sum, 'band', scatter_dimension=1, tiled=True)  52.8 us
    reduce_scatter x1, waiting for transfers between devices, body(): summed = lax.psum_scatter(summed, 'chan', scatter_dimension=0, tiled=True)  34.8 us
  transfers between devices with their start and end apart: 2, of which 2 were waited for; matrix products, arithmetic and copies ran while one was open for 0% of the time, Pallas kernels for 0%

profile of v1, /device:TPU:0, one launch (start us, length us, event | category | flops | bytes accessed | tf_op | source)
XLA Modules:
  0.0 215.7 jit_solution(13916168141612939069)
XLA Ops:
  6.5 0.0 reduce-scatter.3.cloned.1.call-start
  6.5 111.0 %shard_map.17 = f32[1024,1024]{1,0:T(8,128)S(1)} custom-call(bf16[2,8,128,1024]{3,2,1,0:T(8,128)(2,1)} %x_ref.1), custom_call_target="tpu_custom_call" | custom-call | tf_op jit(solution)/shard_map/pallas_call | solution.py:138
  117.5 0.0 copy-start
  117.5 1.9 copy-done
  119.5 0.0 reduce-scatter.3.cloned.1.call-update
  119.5 0.0 reduce-scatter.5.cloned.1.call-start
  119.5 52.8 %reduce-scatter.3.cloned.1.call-done = f32[1024,256]{1,0:T(8,128)} async-done(((f32[1024,1024]{1,0:T(8,128)}), f32[1024,256]{1,0:T(8,128)}) %reduce-scatter.3.cloned.1.call-update) | async-done | bytes 1048592 | tf_op jit(solution)/shard_map/reduce_scatter | solution.py:158
  172.3 0.0 reduce-scatter.5.cloned.1.call-update
  172.4 34.8 %reduce-scatter.5.cloned.1.call-done = f32[128,256]{1,0:T(8,128)} async-done(((f32[1024,256]{1,0:T(8,128)}), f32[128,256]{1,0:T(8,128)}) %reduce-scatter.5.cloned.1.call-update) | async-done | bytes 131088 | tf_op jit(solution)/shard_map/reduce_scatter | solution.py:159
  207.2 1.6 select_multiply_fusion
  (2 shorter events, 0.0 us)
Async XLA Ops:
  6.5 165.8 %reduce-scatter.3.cloned.1.call-start = ((), (), s32[]{:S(2)}) async-start(), calls=%async_computation.2 | async-start | bytes 5242880 | tf_op jit(solution)/shard_map/reduce_scatter | solution.py:158
  117.5 1.9 copy-start
  119.5 87.7 %reduce-scatter.5.cloned.1.call-start = ((), (), s32[]{:S(2)}) async-start(), calls=%async_computation.3 | async-start | bytes 1179648 | tf_op jit(solution)/shard_map/reduce_scatter | solution.py:159
Sparse Core Ops, SparseCore 0:
  119.6 52.6 reduce-scatter.2
  174.6 32.5 reduce-scatter.4
